TPU v7x, 256 devices: a whole 4x4x8 slice. The times are simulated.
256 devices in a mesh: rows: 16 (over z, core), wide: 16 (over y, x).
Axes of the slice: x: 4, y: 4, z: 8, core: 2. Of those that a mesh axis runs over, the one named last changes fastest.
Arguments:
- matrix_tiles: bfloat16 [2048, 16, 128, 128], P('rows', 'wide'), may hold values from -1.5 to 1.5
- row_pointers: int32 [272, 16], P('rows', 'wide'), may hold values from 0 to 112, as said below
- column_blocks: int32 [2048, 16], P('rows', 'wide'), may hold values from 0 to 4095, as said below
- prolongator_tiles: bfloat16 [256, 16, 2, 128, 128], P('rows', 'wide'), may hold values from -0.5 to 0.5
- aggregate_ids: int32 [256, 16, 2], P('rows', 'wide'), may hold values from 0 to 1023, as said below
Outputs:
- coarse_band: bfloat16 [64, 16, 36, 128, 128], P('rows', 'wide')
Inputs may be any that keep to these rules, and one draw needn't show every extreme that they name: `row_pointers`: each device's pointers start at 0 and rise by at least 1 for each of its 16 row blocks; its last pointer, its count of used slots, is at most 112. For two devices with the same rows index whose wide indices differ by 8 the two counts add up to at most 128; in every draw some such pair adds up to exactly 128 and some device holds exactly 112. `column_blocks`: every slot, used or not, names a fine block of its own device, of one of the 4 fine block rows nearest to it on the device beside it along rows, on a device beside it along wide, or on a device beside it along both; the first slot of each row block names that row block. `aggregate_ids`: each names a coarse block owned by the device that owns the fine block: coarse rows 4 r to 4 r + 3 and the same wide index.
All inputs are finite; a program needn't handle non-finite values.
Results may differ from a plain program's by a relative error of at most 0.005.
Values may be sent and summed in bfloat16 or wider, within the bound.
A program may use at most 128 MiB of HBM per device.

v0:
```python
import jax
import jax.numpy as jnp
from jax import lax
from jax.sharding import PartitionSpec as P

TILE = 128
P_TILES = 2
FINE = 16
COARSE = 4
COUPLED_BLOCKS = 4
SLOTS = 128


def extended(block, sides, width):
    for axis, dim in sides:
        count = lax.axis_size(axis)
        forward = [(i, i + 1) for i in range(count - 1)]
        backward = [(target, source) for source, target in forward]
        low = lax.ppermute(
            lax.slice_in_dim(block, block.shape[dim] - width, None, axis=dim), axis, forward
        )
        high = lax.ppermute(lax.slice_in_dim(block, 0, width, axis=dim), axis, backward)
        block = jnp.concatenate([low, block, high], axis=dim)
    return block


def decode(block):
    return block[..., 0].astype(jnp.float32).astype(jnp.int32)


def place_codes(near_row, near_wide):
    step_row = (near_row >= COUPLED_BLOCKS).astype(jnp.int32) + (
        near_row >= COUPLED_BLOCKS + FINE
    ).astype(jnp.int32)
    return step_row * 3 + near_wide


def segments_from(first_c, far_c, code):
    segment = first_c[:, :, None] * (9 * COARSE) + code[:, None, None] * COARSE + far_c[:, None, :]
    return segment.reshape(first_c.shape[0], P_TILES * P_TILES)


def accumulate(own_tiles, own_p, far_p, segment, active, segments):
    slot_total = own_tiles.shape[0]
    block_size = min(32, slot_total)
    block_count = slot_total // block_size

    def split(values):
        return values.reshape((block_count, block_size) + values.shape[1:])

    def add_block(totals, pieces):
        operator, left_p, right_p, block_segment, block_active = pieces
        product = jnp.einsum(
            "sab,smbc->smac", operator, right_p, preferred_element_type=jnp.float32
        ).astype(jnp.bfloat16)
        term_tiles = jnp.einsum(
            "snba,smbc->snmac", left_p, product, preferred_element_type=jnp.float32
        )
        weight = block_active.astype(jnp.float32)[:, None, None, None, None]
        flat_terms = (term_tiles * weight).reshape(block_size * P_TILES * P_TILES, TILE * TILE)
        targets = block_segment.reshape(block_size * P_TILES * P_TILES)
        totals = totals.at[targets].add(flat_terms, mode="drop")
        return (totals, None)

    start = jnp.zeros((segments, TILE * TILE), jnp.float32)
    pieces = (split(own_tiles), split(own_p), split(far_p), split(segment), split(active))
    totals, unused = lax.scan(add_block, start, pieces)
    return totals


def body(matrix_tiles, row_pointers, column_blocks, prolongator_tiles, aggregate_ids):
    wide_count = lax.axis_size("wide")
    row_index = lax.axis_index("rows")
    wide_index = lax.axis_index("wide")
    band_size = 9 * COARSE
    own_segments = COARSE * band_size
    local_c = aggregate_ids[:, 0, :] // wide_count % COARSE
    identity_rows = jnp.broadcast_to(
        local_c.astype(jnp.bfloat16)[:, None, :, None, None], (FINE, 1, P_TILES, 8, TILE)
    )
    transfer_buffer = jnp.concatenate([prolongator_tiles, identity_rows], axis=3)
    boundary_piece = extended(transfer_buffer, (("rows", 0),), COUPLED_BLOCKS)
    rim_all = extended(boundary_piece, (("wide", 1),), 1)
    rim_field = rim_all[:, :, :, :TILE, :]
    rim_c = decode(rim_all[:, :, :, TILE, :])
    pointers = row_pointers[:, 0]
    tile_count = pointers[FINE]
    slot_ids = jnp.arange(SLOTS, dtype=jnp.int32)
    slot_row = jnp.sum((pointers[None, 1:] <= slot_ids[:, None]).astype(jnp.int32), axis=1)
    slot_row = jnp.minimum(slot_row, FINE - 1)
    slot_col = column_blocks[:, 0]
    near_row = jnp.clip(
        slot_col // wide_count - row_index * FINE + COUPLED_BLOCKS, 0, FINE + 2 * COUPLED_BLOCKS - 1
    )
    near_wide = jnp.clip(slot_col % wide_count - wide_index + 1, 0, 2)
    first_c = local_c[slot_row]
    far_c = rim_c[near_row, near_wide]
    code = place_codes(near_row, near_wide)
    segment = segments_from(first_c, far_c, code)
    own_tiles = matrix_tiles[:, 0]
    slot_live = (slot_ids < tile_count).astype(jnp.int32)
    active = slot_live > 0
    own_p = prolongator_tiles[slot_row, 0]
    far_p = rim_field[near_row, near_wide]
    totals = accumulate(own_tiles, own_p, far_p, segment, active, own_segments)
    return totals.astype(jnp.bfloat16).reshape(COARSE, 1, band_size, TILE, TILE)


def solution(mesh):
    placed = (
        P("rows", "wide", None, None),
        P("rows", "wide"),
        P("rows", "wide"),
        P("rows", "wide", None, None, None),
        P("rows", "wide", None),
    )
    return jax.shard_map(
        body,
        mesh=mesh,
        in_specs=placed,
        out_specs=P("rows", "wide", None, None, None),
        check_vma=False,
    )
```

profile of v0, /device:TPU:111, one launch (start us, length us, event | category | flops | bytes accessed | tf_op | source)
XLA Modules:
  0.0 259.4 jit_solution(6792130367295503273)
XLA Ops:
  2.1 5.3 %collective-permute-start = (bf16[4,1,2,136,128]{4,3,2,1,0:T(8,128)(2,1)S(1)}, bf16[4,1,2,136,128]{4,3,2,1,0:T(8,128)(2,1)S(1)}, u32[]{:S(2)}, u32[]{:S(2)}) collective-permute-start(bf16[4,1,2,136,128]{4,3,2,1,0:T(8,128)(2,1)S(1)} %get-tuple-element.94), channel_id=1, source_target_pairs={{0,16},{16,32},{32,48},{48,64},{64,80},{80,96},{96,112},{112,128},... | collective-permute-start | bytes 835592 | tf_op jit(solution)/shard_map/ppermute | solution.py:19
  10.9 5.6 %collective-permute-done.1 = bf16[4,1,2,136,128]{4,3,2,1,0:T(8,128)(2,1)S(1)} collective-permute-done((bf16[4,1,2,136,128]{4,3,2,1,0:T(8,128)(2,1)S(1)}, bf16[4,1,2,136,128]{4,3,2,1,0:T(8,128)(2,1)S(1)}, u32[]{:S(2)}, u32[]{:S(2)}) %collective-permute-start.1) | collective-permute-done | bytes 278560 | tf_op jit(solution)/shard_map/ppermute | solution.py:22
  21.5 4.9 %collective-permute-start.2 = (bf16[24,1,2,136,128]{4,3,2,1,0:T(8,128)(2,1)}, bf16[24,1,2,136,128]{4,3,2,1,0:T(8,128)(2,1)}, u32[]{:S(2)}, u32[]{:S(2)}) collective-permute-start(bf16[24,1,2,136,128]{4,3,2,1,0:T(8,128)(2,1)} %pad_maximum_fusion.5), channel_id=1, source_target_pairs={{0,1},{1,2},{2,3},{3,4},{4,5},{5,6},{6,7},{7,8},{8,9},{9,10},{10,1... | collective-permute-start | bytes 5013512 | tf_op jit(solution)/shard_map/ppermute | solution.py:19
  29.2 6.6 %gather_fusion.3 = bf16[128,2,128,128]{3,2,1,0:T(8,128)(2,1)} fusion(bf16[16,1,2,128,128]{4,3,2,1,0:T(8,128)(2,1)S(1)} %copy-done, s32[128]{0:T(128)S(1)} %get-tuple-element.96), kind=kCustom, calls=%fused_computation.3 | custom fusion | bytes 16778240 | tf_op jit(solution)/shard_map/gather | solution.py:103
  36.4 21.4 %collective-permute-done.3 = bf16[24,1,2,136,128]{4,3,2,1,0:T(8,128)(2,1)S(1)} collective-permute-done((bf16[24,1,2,136,128]{4,3,2,1,0:T(8,128)(2,1)}, bf16[24,1,2,136,128]{4,3,2,1,0:T(8,128)(2,1)S(1)}, u32[]{:S(2)}, u32[]{:S(2)}) %collective-permute-start.3) | collective-permute-done | bytes 1671200 | tf_op jit(solution)/shard_map/ppermute | solution.py:22
  60.6 2.6 %copy.57 = bf16[24,3,2,1,128]{2,0,1,4,3:T(8,128)(2,1)} copy(bf16[24,3,2,1,128]{4,3,2,1,0:T(2,128)(2,1)S(1)} %pad_maximum_fusion.8) | data formatting | bytes 73728
  65.3 5.6 %pad_maximum_fusion = bf16[24,3,2,128,128]{4,3,2,1,0:T(8,128)(2,1)} fusion(bf16[24,1,2,136,128]{4,3,2,1,0:T(8,128)(2,1)S(1)} %collective-permute-done.3, bf16[24,1,2,136,128]{4,3,2,1,0:T(8,128)(2,1)} %collective-permute-done.2, bf16[4,1,2,136,128]{4,3,2,1,0:T(8,128)(2,1)S(1)} %collective-permute-done.1, ...), kind=kLoop, calls=%fused_computation.24 | loop fusion | flops 28311552 | bytes 9732096 | tf_op jit(solution)/shard_map/concatenate | solution.py:23
  70.9 9.6 %gather_fusion.2 = bf16[128,2,128,128]{3,2,1,0:T(8,128)(2,1)} fusion(bf16[24,3,2,128,128]{4,3,2,1,0:T(8,128)(2,1)} %pad_maximum_fusion, s32[128]{0:T(128)S(1)} %fusion.40), kind=kCustom, calls=%fused_computation.2 | custom fusion | bytes 16778240 | tf_op jit(solution)/shard_map/gather | solution.py:104
  80.5 4.6 %broadcast_in_dim.4 = f32[144,16384]{1,0:T(8,128)} broadcast(f32[]{:T(128)} %constant.86.clone.1), dimensions={} | broadcast | bytes 9437188 | tf_op jit(solution)/shard_map/broadcast_in_dim | solution.py:65
  85.2 166.0 %while.10 = (s32[]{:T(128)}, f32[144,16384]{1,0:T(8,128)}, s32[4,32,4]{1,0,2:T(4,128)S(1)}, bf16[4,32,2,128,128]{4,3,2,1,0:T(8,128)(2,1)}, bf16[4,32,128,128]{3,...) while((s32[]{:T(128)}, f32[144,16384]{1,0:T(8,128)}, ...), condition=%wide.region_3.4_spmd, body=%wide.region_1.3_spmd.sunk | while | flops 810549696 | bytes 48240516 | solution.py:67
  85.4 7.7 %multiply_bitcast_fusion.2 = f32[32,2,2,128,128]{3,4,1,2,0:T(8,128)} fusion(f32[32]{0:T(128)S(1)} %fusion.57, bf16[4,32,2,128,128]{4,3,2,1,0:T(8,128)(2,1)} %get-tuple-element.162, s32[]{:T(128)S(6)} %copy.73, bf16[4,32,2,128,128]{4,3,2,1,0:T(8,128)(2,1)} %get-tuple-element.160, bf16[4,32,128,128]{3,2,1,0:T(8,128)(2,1)} %get-tuple-element.161), kind=kOutput, calls=%fused_computation.8.clone.1 | convolution fusion | flops 808452096 | bytes 13633152 | tf_op jit(solution)/shard_map/while/body/eval_jaxpr/snba,smbc->snmac/dot_general | solution.py:56
  93.1 9.0 %copy.69 = f32[32,2,2,128,128]{4,3,2,1,0:T(8,128)} copy(f32[32,2,2,128,128]{3,4,1,2,0:T(8,128)} %multiply_bitcast_fusion.2) | data formatting | bytes 16777216 | tf_op jit(solution)/shard_map/while/body/eval_jaxpr/mul | solution.py:60
  102.0 24.6 %scatter_custom_fusion.5 = f32[144,16384]{1,0:T(8,128)} fusion(f32[144,16384]{1,0:T(8,128)} %get-tuple-element.150, s32[128]{0:T(128)S(1)} %fusion.56, f32[16,8,128,128]{3,2,1,0:T(8,128)} %bitcast.100), kind=kCustom, calls=%fused_computation.5.clone.1 | custom fusion | flops 2097152 | bytes 17825792 | tf_op jit(solution)/shard_map/while/body/eval_jaxpr/scatter-add | solution.py:62
  126.9 7.7 %multiply_bitcast_fusion.2 = f32[32,2,2,128,128]{3,4,1,2,0:T(8,128)} fusion(f32[32]{0:T(128)S(1)} %fusion.57, bf16[4,32,2,128,128]{4,3,2,1,0:T(8,128)(2,1)} %get-tuple-element.162, s32[]{:T(128)S(6)} %copy.73, bf16[4,32,2,128,128]{4,3,2,1,0:T(8,128)(2,1)} %get-tuple-element.160, bf16[4,32,128,128]{3,2,1,0:T(8,128)(2,1)} %get-tuple-element.161), kind=kOutput, calls=%fused_computation.8.clone.1 | convolution fusion | flops 808452096 | bytes 13633152 | tf_op jit(solution)/shard_map/while/body/eval_jaxpr/snba,smbc->snmac/dot_general | solution.py:56
  134.6 9.0 %copy.69 = f32[32,2,2,128,128]{4,3,2,1,0:T(8,128)} copy(f32[32,2,2,128,128]{3,4,1,2,0:T(8,128)} %multiply_bitcast_fusion.2) | data formatting | bytes 16777216 | tf_op jit(solution)/shard_map/while/body/eval_jaxpr/mul | solution.py:60
  143.5 24.6 %scatter_custom_fusion.5 = f32[144,16384]{1,0:T(8,128)} fusion(f32[144,16384]{1,0:T(8,128)} %get-tuple-element.150, s32[128]{0:T(128)S(1)} %fusion.56, f32[16,8,128,128]{3,2,1,0:T(8,128)} %bitcast.100), kind=kCustom, calls=%fused_computation.5.clone.1 | custom fusion | flops 2097152 | bytes 17825792 | tf_op jit(solution)/shard_map/while/body/eval_jaxpr/scatter-add | solution.py:62
  168.4 7.7 %multiply_bitcast_fusion.2 = f32[32,2,2,128,128]{3,4,1,2,0:T(8,128)} fusion(f32[32]{0:T(128)S(1)} %fusion.57, bf16[4,32,2,128,128]{4,3,2,1,0:T(8,128)(2,1)} %get-tuple-element.162, s32[]{:T(128)S(6)} %copy.73, bf16[4,32,2,128,128]{4,3,2,1,0:T(8,128)(2,1)} %get-tuple-element.160, bf16[4,32,128,128]{3,2,1,0:T(8,128)(2,1)} %get-tuple-element.161), kind=kOutput, calls=%fused_computation.8.clone.1 | convolution fusion | flops 808452096 | bytes 13633152 | tf_op jit(solution)/shard_map/while/body/eval_jaxpr/snba,smbc->snmac/dot_general | solution.py:56
  176.1 9.0 %copy.69 = f32[32,2,2,128,128]{4,3,2,1,0:T(8,128)} copy(f32[32,2,2,128,128]{3,4,1,2,0:T(8,128)} %multiply_bitcast_fusion.2) | data formatting | bytes 16777216 | tf_op jit(solution)/shard_map/while/body/eval_jaxpr/mul | solution.py:60
  185.1 24.6 %scatter_custom_fusion.5 = f32[144,16384]{1,0:T(8,128)} fusion(f32[144,16384]{1,0:T(8,128)} %get-tuple-element.150, s32[128]{0:T(128)S(1)} %fusion.56, f32[16,8,128,128]{3,2,1,0:T(8,128)} %bitcast.100), kind=kCustom, calls=%fused_computation.5.clone.1 | custom fusion | flops 2097152 | bytes 17825792 | tf_op jit(solution)/shard_map/while/body/eval_jaxpr/scatter-add | solution.py:62
  209.9 7.7 %multiply_bitcast_fusion.2 = f32[32,2,2,128,128]{3,4,1,2,0:T(8,128)} fusion(f32[32]{0:T(128)S(1)} %fusion.57, bf16[4,32,2,128,128]{4,3,2,1,0:T(8,128)(2,1)} %get-tuple-element.162, s32[]{:T(128)S(6)} %copy.73, bf16[4,32,2,128,128]{4,3,2,1,0:T(8,128)(2,1)} %get-tuple-element.160, bf16[4,32,128,128]{3,2,1,0:T(8,128)(2,1)} %get-tuple-element.161), kind=kOutput, calls=%fused_computation.8.clone.1 | convolution fusion | flops 808452096 | bytes 13633152 | tf_op jit(solution)/shard_map/while/body/eval_jaxpr/snba,smbc->snmac/dot_general | solution.py:56
  217.6 9.0 %copy.69 = f32[32,2,2,128,128]{4,3,2,1,0:T(8,128)} copy(f32[32,2,2,128,128]{3,4,1,2,0:T(8,128)} %multiply_bitcast_fusion.2) | data formatting | bytes 16777216 | tf_op jit(solution)/shard_map/while/body/eval_jaxpr/mul | solution.py:60
  226.6 24.6 %scatter_custom_fusion.5 = f32[144,16384]{1,0:T(8,128)} fusion(f32[144,16384]{1,0:T(8,128)} %get-tuple-element.150, s32[128]{0:T(128)S(1)} %fusion.56, f32[16,8,128,128]{3,2,1,0:T(8,128)} %bitcast.100), kind=kCustom, calls=%fused_computation.5.clone.1 | custom fusion | flops 2097152 | bytes 17825792 | tf_op jit(solution)/shard_map/while/body/eval_jaxpr/scatter-add | solution.py:62
  251.2 4.6 %convert_bitcast_fusion = bf16[18,8,128,128]{3,1,2,0:T(8,128)(2,1)S(1)} fusion(f32[144,16384]{1,0:T(8,128)} %get-tuple-element.42), kind=kLoop, calls=%fused_computation.29 | loop fusion | flops 2359296 | bytes 14155776
  255.8 3.6 %copy.59 = bf16[18,8,128,128]{3,2,1,0:T(8,128)(2,1)} copy(bf16[18,8,128,128]{3,1,2,0:T(8,128)(2,1)S(1)} %convert_bitcast_fusion) | data formatting | bytes 9437184
  (50 shorter events, 19.6 us)
Async XLA Ops:
  0.0 29.2 %copy-start = (bf16[16,1,2,128,128]{4,3,2,1,0:T(8,128)(2,1)S(1)}, bf16[16,1,2,128,128]{4,3,2,1,0:T(8,128)(2,1)}, u32[]{:S(2)}) copy-start(bf16[16,1,2,128,128]{4,3,2,1,0:T(8,128)(2,1)} %param.10) | copy-start | bytes 3145732
  2.1 8.8 %collective-permute-start = (bf16[4,1,2,136,128]{4,3,2,1,0:T(8,128)(2,1)S(1)}, bf16[4,1,2,136,128]{4,3,2,1,0:T(8,128)(2,1)S(1)}, u32[]{:S(2)}, u32[]{:S(2)}) collective-permute-start(bf16[4,1,2,136,128]{4,3,2,1,0:T(8,128)(2,1)S(1)} %get-tuple-element.94), channel_id=1, source_target_pairs={{0,16},{16,32},{32,48},{48,64},{64,80},{80,96},{96,112},{112,128},... | collective-permute-start | bytes 835592 | tf_op jit(solution)/shard_map/ppermute | solution.py:19
  7.4 9.1 %collective-permute-start.1 = (bf16[4,1,2,136,128]{4,3,2,1,0:T(8,128)(2,1)S(1)}, bf16[4,1,2,136,128]{4,3,2,1,0:T(8,128)(2,1)S(1)}, u32[]{:S(2)}, u32[]{:S(2)}) collective-permute-start(bf16[4,1,2,136,128]{4,3,2,1,0:T(8,128)(2,1)S(1)} %get-tuple-element.95), channel_id=1, source_target_pairs={{16,0},{32,16},{48,32},{64,48},{80,64},{96,80},{112,96},{128,112},... | collective-permute-start | bytes 835592 | tf_op jit(solution)/shard_map/ppermute | solution.py:22
  19.0 38.8 %collective-permute-start.3 = (bf16[24,1,2,136,128]{4,3,2,1,0:T(8,128)(2,1)}, bf16[24,1,2,136,128]{4,3,2,1,0:T(8,128)(2,1)S(1)}, u32[]{:S(2)}, u32[]{:S(2)}) collective-permute-start(bf16[24,1,2,136,128]{4,3,2,1,0:T(8,128)(2,1)} %pad_maximum_fusion.5), channel_id=1, source_target_pairs={{1,0},{2,1},{3,2},{4,3},{5,4},{6,5},{7,6},{8,7},{9,8},{10,9},{11,1... | collective-permute-start | bytes 5013512 | tf_op jit(solution)/shard_map/ppermute | solution.py:22
  21.5 38.2 %collective-permute-start.2 = (bf16[24,1,2,136,128]{4,3,2,1,0:T(8,128)(2,1)}, bf16[24,1,2,136,128]{4,3,2,1,0:T(8,128)(2,1)}, u32[]{:S(2)}, u32[]{:S(2)}) collective-permute-start(bf16[24,1,2,136,128]{4,3,2,1,0:T(8,128)(2,1)} %pad_maximum_fusion.5), channel_id=1, source_target_pairs={{0,1},{1,2},{2,3},{3,4},{4,5},{5,6},{6,7},{7,8},{8,9},{9,10},{10,1... | collective-permute-start | bytes 5013512 | tf_op jit(solution)/shard_map/ppermute | solution.py:19
  29.2 7.1 %copy-start.1 = (s32[128,1]{0,1:T(1,128)S(1)}, s32[128,1]{0,1:T(1,128)}, u32[]{:S(2)}) copy-start(s32[128,1]{0,1:T(1,128)} %param.9) | copy-start | bytes 1540
where the time goes:
time: 264 us; the launch traced here: 259 us
  other arithmetic  115 us (44%)
  local copies, waits for them, and re-layouts  68.6 us (26%)
  matrix products  30.7 us (12%)
  waiting for transfers between devices  30.4 us (12%)
  starting transfers between devices  14.6 us (6%)
    scatter-add x4, other arithmetic, add_block(): totals = totals.at[targets].add(flat_terms, mode='drop')  98.5 us
    mul x4, local copies, waits for them, and re-layouts, add_block(): term_tiles * weight  35.9 us
    dot_general x4, matrix products, add_block(): jnp.einsum('snba,smbc->snmac', left_p, product, preferred_element_type=jn...  30.7 us
    ppermute x2, waiting for transfers between devices, extended(): lax.ppermute(lax.slice_in_dim(block, 0, width, axis=dim), axis, backward)  27 us
    ppermute x2, starting transfers between devices, extended(): lax.ppermute(lax.slice_in_dim(block, block.shape[dim] - width, None, axis...  10.3 us
    gather x1, local copies, waits for them, and re-layouts, body(): far_p = rim_field[near_row, near_wide]  9.61 us
    concatenate x2, other arithmetic, extended(): block = jnp.concatenate([low, block, high], axis=dim)  8.18 us
    gather x1, local copies, waits for them, and re-layouts, body(): own_p = prolongator_tiles[slot_row, 0]  6.58 us
  transfers between devices with their start and end apart: 4, of which 4 were waited for; matrix products, arithmetic and copies ran while one was open for 4% of the time, Pallas kernels for 0%

commit v1 on v0

v1 whole, which is shorter than its diff:
```python
import functools

import jax
import jax.numpy as jnp
from jax import lax
from jax.experimental import pallas as pl
from jax.experimental.pallas import tpu as pltpu
from jax.sharding import PartitionSpec as P

TILE = 128
P_TILES = 2
FINE = 16
COARSE = 4
HALO = 4
SLOTS = 128
LIVE = 112
SPAN = FINE + 2 * HALO
WIDE_M = COARSE * TILE
CHUNK_ORDER = (0, 3, 1, 2)
MESH = pl.DeviceIdType.MESH
ROWS_M, ROWS_P = 0, 1


def exact_log2(n):
    bits = n.bit_length() - 1
    assert 1 << bits == n
    return bits


def kernel(
    n_rows,
    n_wide,
    ptr_ref,
    ids_ref,
    col_ref,
    a_hbm,
    p_hbm,
    out_ref,
    a_v,
    ext,
    ext_id,
    own_t,
    r_v,
    phat,
    acc,
    racc,
    meta_v,
    meta_s,
    load_sem,
    meta_sem,
    wide_send,
    wide_recv,
    wid_send,
    wid_recv,
    halo_send,
    halo_recv,
    hid_send,
    hid_recv,
):
    f32, bf16, i32 = jnp.float32, jnp.bfloat16, jnp.int32
    r = lax.axis_index("rows")
    w = lax.axis_index("wide")
    row_peer = (lax.rem(r + n_rows - 1, n_rows), lax.rem(r + 1, n_rows))
    wide_peer = (lax.rem(w + n_wide - 1, n_wide), lax.rem(w + 1, n_wide))
    wide_bits = exact_log2(n_wide)

    barrier = pltpu.get_barrier_semaphore()
    for peer in row_peer:
        pl.semaphore_signal(barrier, inc=1, device_id=(peer, w), device_id_type=MESH)
    for peer in wide_peer:
        pl.semaphore_signal(barrier, inc=1, device_id=(r, peer), device_id_type=MESH)

    loads = []
    own_load = pltpu.make_async_copy(p_hbm.at[:, 0], ext.at[1, pl.ds(HALO, FINE)], load_sem.at[0])
    own_load.start()
    for q in range(4):
        part = pl.ds(q * (LIVE // 4), LIVE // 4)
        load = pltpu.make_async_copy(a_hbm.at[part, 0], a_v.at[part], load_sem.at[1 + q])
        load.start()
        loads.append(load)

    for i in range(FINE):
        for m in range(P_TILES):
            local = lax.shift_right_logical(ids_ref[m, i], wide_bits) & (COARSE - 1)
            ext_id[1, pl.ds((HALO + i) * P_TILES + m, 1), :] = jnp.full((1, TILE), local, i32).astype(f32)

    pl.semaphore_wait(barrier, 4)

    def to_wide(d, chunk):
        side = 0 if d == 1 else 2
        return pltpu.make_async_remote_copy(
            src_ref=p_hbm.at[pl.ds(chunk * HALO, HALO), 0],
            dst_ref=ext.at[side, pl.ds(HALO + chunk * HALO, HALO)],
            send_sem=wide_send.at[d, chunk],
            recv_sem=wide_recv.at[d, chunk],
            device_id=(r, wide_peer[d]),
            device_id_type=MESH,
        )

    def to_wide_id(d):
        side = 0 if d == 1 else 2
        part = pl.ds(HALO * P_TILES, FINE * P_TILES)
        return pltpu.make_async_remote_copy(
            src_ref=ext_id.at[1, part],
            dst_ref=ext_id.at[side, part],
            send_sem=wid_send.at[d],
            recv_sem=wid_recv.at[d],
            device_id=(r, wide_peer[d]),
            device_id_type=MESH,
        )

    def to_rows(d, side):
        source = FINE if d == 1 else HALO
        target = 0 if d == 1 else HALO + FINE
        if side == 1:
            src = p_hbm.at[pl.ds(source - HALO, HALO), 0]
        else:
            src = ext.at[side, pl.ds(source, HALO)]
        return pltpu.make_async_remote_copy(
            src_ref=src,
            dst_ref=ext.at[side, pl.ds(target, HALO)],
            send_sem=halo_send.at[d, side],
            recv_sem=halo_recv.at[d, side],
            device_id=(row_peer[d], w),
            device_id_type=MESH,
        )

    def to_rows_id(d, side):
        source = FINE if d == 1 else HALO
        target = 0 if d == 1 else HALO + FINE
        return pltpu.make_async_remote_copy(
            src_ref=ext_id.at[side, pl.ds(source * P_TILES, HALO * P_TILES)],
            dst_ref=ext_id.at[side, pl.ds(target * P_TILES, HALO * P_TILES)],
            send_sem=hid_send.at[d, side],
            recv_sem=hid_recv.at[d, side],
            device_id=(row_peer[d], w),
            device_id_type=MESH,
        )

    for chunk in CHUNK_ORDER:
        for d in (0, 1):
            to_wide(d, chunk).start()
        if chunk == 0:
            for d in (0, 1):
                to_rows(d, 1).start()

    lane = lax.broadcasted_iota(i32, (TILE, SLOTS), 1)
    sub = lax.broadcasted_iota(i32, (TILE, SLOTS), 0)
    col = jnp.broadcast_to(col_ref[...], (TILE, SLOTS))
    near_row = lax.shift_right_logical(col, wide_bits) - r * FINE + HALO
    near_wide = (col & (n_wide - 1)) - w + 1
    key_l = jnp.where(lane < ptr_ref[FINE], near_wide * SPAN + near_row, 3 * SPAN)
    row_l = jnp.zeros((TILE, SLOTS), i32)
    for k in range(1, FINE):
        row_l = row_l + (lane >= ptr_ref[k]).astype(i32)
    key_s = key_l.T
    row_s = row_l.T
    same = key_s == key_l
    ahead = (key_s < key_l) | (same & (sub < lane))
    rank_l = jnp.sum(ahead.astype(i32), axis=0, keepdims=True)
    later_l = jnp.sum((same & (sub < lane)).astype(i32), axis=0, keepdims=True)
    rank_s = jnp.broadcast_to(rank_l, (TILE, SLOTS)).T
    later_s = jnp.broadcast_to(later_l, (TILE, SLOTS)).T
    chosen = rank_s == lane

    def pick(values):
        return jnp.sum(jnp.where(chosen, values, 0), axis=0, keepdims=True)

    upto = jnp.sum((key_s <= lane).astype(i32), axis=0, keepdims=True)
    count = jnp.sum((key_s == lane).astype(i32), axis=0, keepdims=True)
    meta_v[0:1, :] = pick(sub)
    meta_v[1:2, :] = pick(row_s)
    meta_v[2:3, :] = pick((later_s > 0).astype(i32))
    meta_v[3:4, :] = jnp.where(count > 0, upto - 1, LIVE)
    meta_v[4:8, :] = jnp.zeros((4, TILE), i32)
    r_v[LIVE] = jnp.zeros((WIDE_M, TILE), bf16)
    racc[...] = jnp.zeros((WIDE_M, TILE), f32)

    own_load.wait()

    def id_mask(side, index, c):
        return (ext_id[side, pl.ds(index, 1), :] == jnp.float32(c)).astype(f32).astype(bf16)

    for d in (0, 1):
        to_wide_id(d).start()
        to_rows_id(d, 1).start()

    @pl.loop(0, FINE)
    def _(i):
        first = ext[1, HALO + i, 0].T
        second = ext[1, HALO + i, 1].T
        for c in range(COARSE):
            own_t[i, c * TILE : (c + 1) * TILE, :] = first * id_mask(1, (HALO + i) * P_TILES, c) + second * id_mask(
                1, (HALO + i) * P_TILES + 1, c
            )

    meta_copy = pltpu.make_async_copy(meta_v, meta_s, meta_sem)
    meta_copy.start()
    meta_copy.wait()
    for load in loads:
        load.wait()

    @pl.loop(0, LIVE)
    def _(k):
        tile = a_v[jnp.clip(meta_s[0, k], 0, LIVE - 1)]
        left = own_t[jnp.clip(meta_s[1, k], 0, FINE - 1)]
        keep = meta_s[2, k].astype(f32)
        total = racc[...] * keep + jnp.dot(left, tile, preferred_element_type=f32)
        racc[...] = total
        r_v[k] = total.astype(bf16)

    def chunk_product(side, row, slot):
        for l in range(HALO):
            index = (row + l) * P_TILES
            first = ext[side, row + l, 0]
            second = ext[side, row + l, 1]
            for c in range(COARSE):
                phat[slot, l * TILE : (l + 1) * TILE, c * TILE : (c + 1) * TILE] = first * id_mask(
                    side, index, c
                ) + second * id_mask(side, index + 1, c)
        base = side * SPAN + row
        left = jnp.concatenate([r_v[jnp.clip(meta_s[3, base + l], 0, LIVE)] for l in range(HALO)], axis=1)
        return jnp.dot(left, phat[slot], preferred_element_type=f32)

    def put(code, value):
        for c1 in range(COARSE):
            for c2 in range(COARSE):
                out_ref[c1, 0, code * COARSE + c2] = value[
                    c1 * TILE : (c1 + 1) * TILE, c2 * TILE : (c2 + 1) * TILE
                ].astype(bf16)

    acc[1] = chunk_product(1, HALO, 0)

    @pl.loop(1, FINE // HALO - 1)
    def _(q):
        acc[1] += chunk_product(1, HALO + q * HALO, 0)

    put(4, acc[1] + chunk_product(1, FINE, 1))

    for d in (0, 1):
        to_wide_id(d).wait_recv()
        to_wide(d, 0).wait_recv()
        to_rows(0, 0 if d == 1 else 2).start()
        to_rows_id(0, 0 if d == 1 else 2).start()
    for d in (0, 1):
        side = 0 if d == 1 else 2
        acc[side] = chunk_product(side, HALO, d)
    for d in (0, 1):
        to_wide(d, 3).wait_recv()
        to_rows(1, 0 if d == 1 else 2).start()
        to_rows_id(1, 0 if d == 1 else 2).start()
    for d in (0, 1):
        side = 0 if d == 1 else 2
        acc[side] += chunk_product(side, FINE, d)

    for d in (0, 1):
        to_rows(d, 1).wait_recv()
        to_rows_id(d, 1).wait_recv()
        step = 0 if d == 1 else 2
        put(step * 3 + 1, chunk_product(1, 0 if d == 1 else HALO + FINE, d))

    for d in (0, 1):
        side = 0 if d == 1 else 2
        to_wide(d, 1).wait_recv()
        acc[side] += chunk_product(side, 2 * HALO, d)

    for d in (0, 1):
        for side in (0, 2):
            to_rows(d, side).wait_recv()
            to_rows_id(d, side).wait_recv()
            step = 0 if d == 1 else 2
            put(step * 3 + side, chunk_product(side, 0 if d == 1 else HALO + FINE, side // 2))

    for d in (0, 1):
        side = 0 if d == 1 else 2
        to_wide(d, 2).wait_recv()
        put(3 + side, acc[side] + chunk_product(side, 3 * HALO, d))

    for d in (0, 1):
        to_wide_id(d).wait_send()
        for chunk in CHUNK_ORDER:
            to_wide(d, chunk).wait_send()
        for side in (0, 1, 2):
            to_rows(d, side).wait_send()
            to_rows_id(d, side).wait_send()


def body(matrix_tiles, row_pointers, column_blocks, prolongator_tiles, aggregate_ids):
    n_rows, n_wide = lax.axis_size("rows"), lax.axis_size("wide")
    bf16, f32, i32 = jnp.bfloat16, jnp.float32, jnp.int32
    dma = pltpu.SemaphoreType.DMA
    smem = pl.BlockSpec(memory_space=pltpu.SMEM)
    anywhere = pl.BlockSpec(memory_space=pl.ANY)
    vmem = pl.BlockSpec(memory_space=pltpu.VMEM)
    return pl.pallas_call(
        functools.partial(kernel, n_rows, n_wide),
        out_shape=jax.ShapeDtypeStruct((COARSE, 1, 9 * COARSE, TILE, TILE), bf16),
        in_specs=[smem, smem, vmem, anywhere, anywhere],
        out_specs=vmem,
        scratch_shapes=[
            pltpu.VMEM((LIVE, TILE, TILE), bf16),
            pltpu.VMEM((3, SPAN, P_TILES, TILE, TILE), bf16),
            pltpu.VMEM((3, SPAN * P_TILES, TILE), f32),
            pltpu.VMEM((FINE, WIDE_M, TILE), bf16),
            pltpu.VMEM((LIVE + 1, WIDE_M, TILE), bf16),
            pltpu.VMEM((2, HALO * TILE, WIDE_M), bf16),
            pltpu.VMEM((3, WIDE_M, WIDE_M), f32),
            pltpu.VMEM((WIDE_M, TILE), f32),
            pltpu.VMEM((8, TILE), i32),
            pltpu.SMEM((8, TILE), i32),
            dma((5,)),
            dma,
            dma((2, 4)),
            dma((2, 4)),
            dma((2,)),
            dma((2,)),
            dma((2, 3)),
            dma((2, 3)),
            dma((2, 3)),
            dma((2, 3)),
        ],
        compiler_params=pltpu.CompilerParams(
            collective_id=0, has_side_effects=True, vmem_limit_bytes=56 * 1024 * 1024
        ),
        name="galerkin",
    )(
        row_pointers.reshape(FINE + 1),
        aggregate_ids.transpose(1, 2, 0).reshape(P_TILES, FINE),
        column_blocks.reshape(1, SLOTS),
        matrix_tiles,
        prolongator_tiles,
    )


def solution(mesh):
    placed = (
        P("rows", "wide", None, None),
        P("rows", "wide"),
        P("rows", "wide"),
        P("rows", "wide", None, None, None),
        P("rows", "wide", None),
    )
    return jax.shard_map(
        body,
        mesh=mesh,
        in_specs=placed,
        out_specs=P("rows", "wide", None, None, None),
        check_vma=False,
    )
```

time: 264 us -> 53.3 us (0.20)
  the two profiles are of different devices: /device:TPU:111 before, /device:TPU:2 now
where the time goes in v1:
time: 53.3 us; the launch traced here: 53.2 us
  Pallas kernels  46.8 us (88%)
  local copies, waits for them, and re-layouts  6.36 us (12%)
    pallas_call x1, Pallas kernels, body(): pl.pallas_call(functools.partial(kernel, n_rows, n_wide), out_shape=jax.S...  46.8 us
    unnamed x1, local copies, waits for them, and re-layouts  6.36 us

profile of v1, /device:TPU:2, one launch (start us, length us, event | category | flops | bytes accessed | tf_op | source)
XLA Modules:
  0.0 53.2 jit_solution(779726709186252969)
XLA Ops:
  0.0 46.8 %galerkin.1 = bf16[4,1,36,128,128]{4,3,2,1,0:T(8,128)(2,1)} custom-call(s32[17]{0:T(128)} %bitcast.6, s32[2,16]{1,0:T(2,128)} %bitcast.5, s32[1,128]{1,0:T(1,128)} %bitcast.7, bf16[128,1,128,128]{3,2,1,0:T(8,128)(2,1)} %a_hbm.1, bf16[16,1,2,128,128]{4,3,2,1,0:T(8,128)(2,1)} %p_hbm.1), custom_call_target="tpu_custom_call" | custom-call | tf_op jit(solution)/shard_map/galerkin/pallas_call | solution.py:295
  46.8 6.4 %copy.7 = bf16[4,1,36,128,128]{4,3,2,1,0:T(8,128)(2,1)} copy(bf16[4,1,36,128,128]{4,3,2,1,0:T(8,128)(2,1)} %galerkin.1) | data formatting | bytes 9437184

commit v2 on v1

--- a/solution.py
+++ b/solution.py
@@ -142,6 +142,8 @@
             to_wide(d, chunk).start()
         if chunk == 0:
             for d in (0, 1):
+                to_wide_id(d).start()
+                to_rows_id(d, 1).start()
                 to_rows(d, 1).start()
 
     lane = lax.broadcasted_iota(i32, (TILE, SLOTS), 1)
@@ -181,10 +183,6 @@
     def id_mask(side, index, c):
         return (ext_id[side, pl.ds(index, 1), :] == jnp.float32(c)).astype(f32).astype(bf16)
 
-    for d in (0, 1):
-        to_wide_id(d).start()
-        to_rows_id(d, 1).start()
-
     @pl.loop(0, FINE)
     def _(i):
         first = ext[1, HALO + i, 0].T
@@ -200,7 +198,7 @@
     for load in loads:
         load.wait()
 
-    @pl.loop(0, LIVE)
+    @pl.loop(0, LIVE, unroll=8)
     def _(k):
         tile = a_v[jnp.clip(meta_s[0, k], 0, LIVE - 1)]
         left = own_t[jnp.clip(meta_s[1, k], 0, FINE - 1)]
@@ -290,11 +288,11 @@
     bf16, f32, i32 = jnp.bfloat16, jnp.float32, jnp.int32
     dma = pltpu.SemaphoreType.DMA
     smem = pl.BlockSpec(memory_space=pltpu.SMEM)
-    anywhere = pl.BlockSpec(memory_space=pl.ANY)
+    anywhere = pl.BlockSpec(memory_space=pltpu.HBM)
     vmem = pl.BlockSpec(memory_space=pltpu.VMEM)
     return pl.pallas_call(
         functools.partial(kernel, n_rows, n_wide),
-        out_shape=jax.ShapeDtypeStruct((COARSE, 1, 9 * COARSE, TILE, TILE), bf16),
+        out_shape=pltpu.VMEM((COARSE, 1, 9 * COARSE, TILE, TILE), bf16),
         in_specs=[smem, smem, vmem, anywhere, anywhere],
         out_specs=vmem,
         scratch_shapes=[
@@ -320,7 +318,7 @@
             dma((2, 3)),
         ],
         compiler_params=pltpu.CompilerParams(
-            collective_id=0, has_side_effects=True, vmem_limit_bytes=56 * 1024 * 1024
+            collective_id=0, has_side_effects=True, vmem_limit_bytes=57344 * 1024
         ),
         name="galerkin",
     )(

time: 53.3 us -> 34.7 us (0.65)
  the two profiles are of different devices: /device:TPU:2 before, /device:TPU:65 now
where the time goes in v2:
time: 34.7 us; the launch traced here: 34.6 us
  Pallas kernels  32.4 us (93%)
  local copies, waits for them, and re-layouts  2.19 us (6%)
    pallas_call x1, Pallas kernels, body(): pl.pallas_call(functools.partial(kernel, n_rows, n_wide), out_shape=pltpu...  32.4 us
    unnamed x1, local copies, waits for them, and re-layouts  2.19 us

profile of v2, /device:TPU:65, one launch (start us, length us, event | category | flops | bytes accessed | tf_op | source)
XLA Modules:
  0.0 34.6 jit_solution(9648340940643509445)
XLA Ops:
  0.0 32.4 %galerkin.1 = bf16[4,1,36,128,128]{4,3,2,1,0:T(8,128)(2,1)S(1)} custom-call(s32[17]{0:T(128)} %bitcast.6, s32[2,16]{1,0:T(2,128)} %bitcast.5, s32[1,128]{1,0:T(1,128)} %bitcast.7, bf16[128,1,128,128]{3,2,1,0:T(8,128)(2,1)} %a_hbm.1, bf16[16,1,2,128,128]{4,3,2,1,0:T(8,128)(2,1)} %p_hbm.1), custom_call_target="tpu_custom_call" | custom-call | tf_op jit(solution)/shard_map/galerkin/pallas_call | solution.py:293
  32.4 2.2 %copy.7 = bf16[4,1,36,128,128]{4,3,2,1,0:T(8,128)(2,1)} copy(bf16[4,1,36,128,128]{4,3,2,1,0:T(8,128)(2,1)S(1)} %galerkin.1) | data formatting | bytes 9437184

commit v3 on v2

--- a/solution.py
+++ b/solution.py
@@ -16,9 +16,8 @@
 LIVE = 112
 SPAN = FINE + 2 * HALO
 WIDE_M = COARSE * TILE
-CHUNK_ORDER = (0, 3, 1, 2)
+PIECES = ((0, 4), (12, 4), (4, 4), (8, 2), (10, 2))
 MESH = pl.DeviceIdType.MESH
-ROWS_M, ROWS_P = 0, 1
 
 
 def exact_log2(n):
@@ -60,15 +59,21 @@
     f32, bf16, i32 = jnp.float32, jnp.bfloat16, jnp.int32
     r = lax.axis_index("rows")
     w = lax.axis_index("wide")
-    row_peer = (lax.rem(r + n_rows - 1, n_rows), lax.rem(r + 1, n_rows))
-    wide_peer = (lax.rem(w + n_wide - 1, n_wide), lax.rem(w + 1, n_wide))
+    row_peer, has_row = (r - 1, r + 1), (r > 0, r < n_rows - 1)
+    wide_peer, has_wide = (w - 1, w + 1), (w > 0, w < n_wide - 1)
+    has_side = {0: has_wide[0], 2: has_wide[1]}
     wide_bits = exact_log2(n_wide)
 
     barrier = pltpu.get_barrier_semaphore()
-    for peer in row_peer:
-        pl.semaphore_signal(barrier, inc=1, device_id=(peer, w), device_id_type=MESH)
-    for peer in wide_peer:
-        pl.semaphore_signal(barrier, inc=1, device_id=(r, peer), device_id_type=MESH)
+    for d in (0, 1):
+
+        @pl.when(has_wide[d])
+        def _():
+            pl.semaphore_signal(barrier, inc=1, device_id=(r, wide_peer[d]), device_id_type=MESH)
+
+        @pl.when(has_row[d])
+        def _():
+            pl.semaphore_signal(barrier, inc=1, device_id=(row_peer[d], w), device_id_type=MESH)
 
     loads = []
     own_load = pltpu.make_async_copy(p_hbm.at[:, 0], ext.at[1, pl.ds(HALO, FINE)], load_sem.at[0])
@@ -84,15 +89,37 @@
             local = lax.shift_right_logical(ids_ref[m, i], wide_bits) & (COARSE - 1)
             ext_id[1, pl.ds((HALO + i) * P_TILES + m, 1), :] = jnp.full((1, TILE), local, i32).astype(f32)
 
-    pl.semaphore_wait(barrier, 4)
-
-    def to_wide(d, chunk):
+    for d in (0, 1):
+        side = 2 * d
+
+        @pl.when(jnp.logical_not(has_wide[d]))
+        def _():
+            ext_id[side] = jnp.zeros((SPAN * P_TILES, TILE), f32)
+
+            @pl.loop(0, SPAN)
+            def _(i):
+                ext[side, i] = jnp.zeros((P_TILES, TILE, TILE), bf16)
+
+        @pl.when(jnp.logical_not(has_row[d]))
+        def _():
+            row = d * (HALO + FINE)
+            for side in (0, 1, 2):
+                ext_id[side, pl.ds(row * P_TILES, HALO * P_TILES), :] = jnp.zeros((HALO * P_TILES, TILE), f32)
+
+                @pl.loop(0, HALO)
+                def _(i):
+                    ext[side, row + i] = jnp.zeros((P_TILES, TILE, TILE), bf16)
+
+    pl.semaphore_wait(barrier, sum(there.astype(i32) for there in has_row + has_wide))
+
+    def to_wide(d, piece):
         side = 0 if d == 1 else 2
+        row, rows = PIECES[piece]
         return pltpu.make_async_remote_copy(
-            src_ref=p_hbm.at[pl.ds(chunk * HALO, HALO), 0],
-            dst_ref=ext.at[side, pl.ds(HALO + chunk * HALO, HALO)],
-            send_sem=wide_send.at[d, chunk],
-            recv_sem=wide_recv.at[d, chunk],
+            src_ref=p_hbm.at[pl.ds(row, rows), 0],
+            dst_ref=ext.at[side, pl.ds(HALO + row, rows)],
+            send_sem=wide_send.at[d, piece],
+            recv_sem=wide_recv.at[d, piece],
             device_id=(r, wide_peer[d]),
             device_id_type=MESH,
         )
@@ -137,14 +164,26 @@
             device_id_type=MESH,
         )
 
-    for chunk in CHUNK_ORDER:
-        for d in (0, 1):
-            to_wide(d, chunk).start()
-        if chunk == 0:
-            for d in (0, 1):
-                to_wide_id(d).start()
-                to_rows_id(d, 1).start()
-                to_rows(d, 1).start()
+    for d in (0, 1):
+
+        @pl.when(has_wide[d])
+        def _():
+            to_wide(d, 0).start()
+            to_wide_id(d).start()
+
+    for d in (0, 1):
+
+        @pl.when(has_row[d])
+        def _():
+            to_rows_id(d, 1).start()
+            to_rows(d, 1).start()
+
+    for d in (0, 1):
+
+        @pl.when(has_wide[d])
+        def _():
+            for piece in range(1, len(PIECES)):
+                to_wide(d, piece).start()
 
     lane = lax.broadcasted_iota(i32, (TILE, SLOTS), 1)
     sub = lax.broadcasted_iota(i32, (TILE, SLOTS), 0)
@@ -207,8 +246,8 @@
         racc[...] = total
         r_v[k] = total.astype(bf16)
 
-    def chunk_product(side, row, slot):
-        for l in range(HALO):
+    def chunk_product(side, row, slot, rows=HALO):
+        for l in range(rows):
             index = (row + l) * P_TILES
             first = ext[side, row + l, 0]
             second = ext[side, row + l, 1]
@@ -217,8 +256,8 @@
                     side, index, c
                 ) + second * id_mask(side, index + 1, c)
         base = side * SPAN + row
-        left = jnp.concatenate([r_v[jnp.clip(meta_s[3, base + l], 0, LIVE)] for l in range(HALO)], axis=1)
-        return jnp.dot(left, phat[slot], preferred_element_type=f32)
+        left = jnp.concatenate([r_v[jnp.clip(meta_s[3, base + l], 0, LIVE)] for l in range(rows)], axis=1)
+        return jnp.dot(left, phat[slot, : rows * TILE, :], preferred_element_type=f32)
 
     def put(code, value):
         for c1 in range(COARSE):
@@ -235,52 +274,96 @@
 
     put(4, acc[1] + chunk_product(1, FINE, 1))
 
-    for d in (0, 1):
-        to_wide_id(d).wait_recv()
-        to_wide(d, 0).wait_recv()
-        to_rows(0, 0 if d == 1 else 2).start()
-        to_rows_id(0, 0 if d == 1 else 2).start()
-    for d in (0, 1):
-        side = 0 if d == 1 else 2
-        acc[side] = chunk_product(side, HALO, d)
-    for d in (0, 1):
-        to_wide(d, 3).wait_recv()
-        to_rows(1, 0 if d == 1 else 2).start()
-        to_rows_id(1, 0 if d == 1 else 2).start()
-    for d in (0, 1):
-        side = 0 if d == 1 else 2
-        acc[side] += chunk_product(side, FINE, d)
-
-    for d in (0, 1):
-        to_rows(d, 1).wait_recv()
-        to_rows_id(d, 1).wait_recv()
+    for step in (0, 1):
+        for d in (0, 1):
+            side = 0 if d == 1 else 2
+
+            @pl.when(has_side[side])
+            def _():
+                if step == 0:
+                    to_wide_id(d).wait_recv()
+                to_wide(d, step).wait_recv()
+
+                @pl.when(has_row[step])
+                def _():
+                    to_rows_id(step, side).start()
+                    to_rows(step, side).start()
+
+        for d in (0, 1):
+            side = 0 if d == 1 else 2
+            value = chunk_product(side, HALO + PIECES[step][0], d)
+            if step == 0:
+                acc[side] = value
+            else:
+                acc[side] += value
+
+    for d in (0, 1):
+
+        @pl.when(has_row[1 - d])
+        def _():
+            to_rows(d, 1).wait_recv()
+            to_rows_id(d, 1).wait_recv()
+
         step = 0 if d == 1 else 2
         put(step * 3 + 1, chunk_product(1, 0 if d == 1 else HALO + FINE, d))
 
     for d in (0, 1):
         side = 0 if d == 1 else 2
-        to_wide(d, 1).wait_recv()
-        acc[side] += chunk_product(side, 2 * HALO, d)
+
+        @pl.when(has_side[side])
+        def _():
+            to_wide(d, 2).wait_recv()
+
+        acc[side] += chunk_product(side, HALO + PIECES[2][0], d)
 
     for d in (0, 1):
         for side in (0, 2):
-            to_rows(d, side).wait_recv()
-            to_rows_id(d, side).wait_recv()
+
+            @pl.when(has_row[1 - d] & has_side[side])
+            def _():
+                to_rows(d, side).wait_recv()
+                to_rows_id(d, side).wait_recv()
+
             step = 0 if d == 1 else 2
             put(step * 3 + side, chunk_product(side, 0 if d == 1 else HALO + FINE, side // 2))
 
     for d in (0, 1):
         side = 0 if d == 1 else 2
-        to_wide(d, 2).wait_recv()
-        put(3 + side, acc[side] + chunk_product(side, 3 * HALO, d))
-
-    for d in (0, 1):
-        to_wide_id(d).wait_send()
-        for chunk in CHUNK_ORDER:
-            to_wide(d, chunk).wait_send()
-        for side in (0, 1, 2):
-            to_rows(d, side).wait_send()
-            to_rows_id(d, side).wait_send()
+
+        @pl.when(has_side[side])
+        def _():
+            to_wide(d, 3).wait_recv()
+
+        acc[side] += chunk_product(side, HALO + PIECES[3][0], d, PIECES[3][1])
+
+    for d in (0, 1):
+        side = 0 if d == 1 else 2
+
+        @pl.when(has_side[side])
+        def _():
+            to_wide(d, 4).wait_recv()
+
+        put(3 + side, acc[side] + chunk_product(side, HALO + PIECES[4][0], d, PIECES[4][1]))
+
+    for d in (0, 1):
+
+        @pl.when(has_wide[d])
+        def _():
+            to_wide_id(d).wait_send()
+            for piece in range(len(PIECES)):
+                to_wide(d, piece).wait_send()
+
+        @pl.when(has_row[d])
+        def _():
+            to_rows(d, 1).wait_send()
+            to_rows_id(d, 1).wait_send()
+
+        for side in (0, 2):
+
+            @pl.when(has_row[d] & has_side[side])
+            def _():
+                to_rows(d, side).wait_send()
+                to_rows_id(d, side).wait_send()
 
 
 def body(matrix_tiles, row_pointers, column_blocks, prolongator_tiles, aggregate_ids):
@@ -308,8 +391,8 @@
             pltpu.SMEM((8, TILE), i32),
             dma((5,)),
             dma,
-            dma((2, 4)),
-            dma((2, 4)),
+            dma((2, len(PIECES))),
+            dma((2, len(PIECES))),
             dma((2,)),
             dma((2,)),
             dma((2, 3)),

time: 34.7 us -> 33.1 us (0.954)
  the two profiles are of different devices: /device:TPU:65 before, /device:TPU:111 now
where the time goes in v3:
time: 33.1 us; the launch traced here: 33 us
  Pallas kernels  30.8 us (93%)
  local copies, waits for them, and re-layouts  2.19 us (7%)
    pallas_call x1, Pallas kernels, body(): pl.pallas_call(functools.partial(kernel, n_rows, n_wide), out_shape=pltpu...  30.8 us
    unnamed x1, local copies, waits for them, and re-layouts  2.19 us

profile of v3, /device:TPU:111, one launch (start us, length us, event | category | flops | bytes accessed | tf_op | source)
XLA Modules:
  0.0 33.0 jit_solution(7843449168260268786)
XLA Ops:
  0.0 30.8 %galerkin.1 = bf16[4,1,36,128,128]{4,3,2,1,0:T(8,128)(2,1)S(1)} custom-call(s32[17]{0:T(128)} %bitcast.6, s32[2,16]{1,0:T(2,128)} %bitcast.5, s32[1,128]{1,0:T(1,128)} %bitcast.7, bf16[128,1,128,128]{3,2,1,0:T(8,128)(2,1)} %a_hbm.1, bf16[16,1,2,128,128]{4,3,2,1,0:T(8,128)(2,1)} %p_hbm.1), custom_call_target="tpu_custom_call" | custom-call | tf_op jit(solution)/shard_map/galerkin/pallas_call | solution.py:376
  30.8 2.2 %copy.7 = bf16[4,1,36,128,128]{4,3,2,1,0:T(8,128)(2,1)} copy(bf16[4,1,36,128,128]{4,3,2,1,0:T(8,128)(2,1)S(1)} %galerkin.1) | data formatting | bytes 9437184

commit v4 on v3

--- a/solution.py
+++ b/solution.py
@@ -38,6 +38,7 @@
     a_v,
     ext,
     ext_id,
+    ids_v,
     own_t,
     r_v,
     phat,
@@ -84,10 +85,14 @@
         load.start()
         loads.append(load)
 
+    id_lane = lax.broadcasted_iota(i32, (8, TILE), 1)
+    id_tile = jnp.zeros((8, TILE), i32)
     for i in range(FINE):
         for m in range(P_TILES):
             local = lax.shift_right_logical(ids_ref[m, i], wide_bits) & (COARSE - 1)
             ext_id[1, pl.ds((HALO + i) * P_TILES + m, 1), :] = jnp.full((1, TILE), local, i32).astype(f32)
+            id_tile = jnp.where(id_lane == i * P_TILES + m, local, id_tile)
+    ids_v[1, 1] = id_tile.astype(f32)
 
     for d in (0, 1):
         side = 2 * d
@@ -110,13 +115,14 @@
                 def _(i):
                     ext[side, row + i] = jnp.zeros((P_TILES, TILE, TILE), bf16)
 
+    own_load.wait()
     pl.semaphore_wait(barrier, sum(there.astype(i32) for there in has_row + has_wide))
 
     def to_wide(d, piece):
         side = 0 if d == 1 else 2
         row, rows = PIECES[piece]
         return pltpu.make_async_remote_copy(
-            src_ref=p_hbm.at[pl.ds(row, rows), 0],
+            src_ref=ext.at[1, pl.ds(HALO + row, rows)],
             dst_ref=ext.at[side, pl.ds(HALO + row, rows)],
             send_sem=wide_send.at[d, piece],
             recv_sem=wide_recv.at[d, piece],
@@ -126,10 +132,9 @@
 
     def to_wide_id(d):
         side = 0 if d == 1 else 2
-        part = pl.ds(HALO * P_TILES, FINE * P_TILES)
         return pltpu.make_async_remote_copy(
-            src_ref=ext_id.at[1, part],
-            dst_ref=ext_id.at[side, part],
+            src_ref=ids_v.at[1, 1],
+            dst_ref=ids_v.at[side, 1],
             send_sem=wid_send.at[d],
             recv_sem=wid_recv.at[d],
             device_id=(r, wide_peer[d]),
@@ -139,12 +144,8 @@
     def to_rows(d, side):
         source = FINE if d == 1 else HALO
         target = 0 if d == 1 else HALO + FINE
-        if side == 1:
-            src = p_hbm.at[pl.ds(source - HALO, HALO), 0]
-        else:
-            src = ext.at[side, pl.ds(source, HALO)]
         return pltpu.make_async_remote_copy(
-            src_ref=src,
+            src_ref=ext.at[side, pl.ds(source, HALO)],
             dst_ref=ext.at[side, pl.ds(target, HALO)],
             send_sem=halo_send.at[d, side],
             recv_sem=halo_recv.at[d, side],
@@ -153,11 +154,9 @@
         )
 
     def to_rows_id(d, side):
-        source = FINE if d == 1 else HALO
-        target = 0 if d == 1 else HALO + FINE
         return pltpu.make_async_remote_copy(
-            src_ref=ext_id.at[side, pl.ds(source * P_TILES, HALO * P_TILES)],
-            dst_ref=ext_id.at[side, pl.ds(target * P_TILES, HALO * P_TILES)],
+            src_ref=ids_v.at[side, 1],
+            dst_ref=ids_v.at[side, 0 if d == 1 else 2],
             send_sem=hid_send.at[d, side],
             recv_sem=hid_recv.at[d, side],
             device_id=(row_peer[d], w),
@@ -217,7 +216,10 @@
     r_v[LIVE] = jnp.zeros((WIDE_M, TILE), bf16)
     racc[...] = jnp.zeros((WIDE_M, TILE), f32)
 
-    own_load.wait()
+    def spread_ids(side, part):
+        table = jnp.broadcast_to(ids_v[side, part, 0:1, :], (TILE, TILE)).T
+        first, count, row = ((FINE - HALO, HALO, 0), (0, FINE, HALO), (0, HALO, HALO + FINE))[part]
+        ext_id[side, pl.ds(row * P_TILES, count * P_TILES), :] = table[first * P_TILES : (first + count) * P_TILES]
 
     def id_mask(side, index, c):
         return (ext_id[side, pl.ds(index, 1), :] == jnp.float32(c)).astype(f32).astype(bf16)
@@ -282,6 +284,7 @@
             def _():
                 if step == 0:
                     to_wide_id(d).wait_recv()
+                    spread_ids(side, 1)
                 to_wide(d, step).wait_recv()
 
                 @pl.when(has_row[step])
@@ -303,6 +306,7 @@
         def _():
             to_rows(d, 1).wait_recv()
             to_rows_id(d, 1).wait_recv()
+            spread_ids(1, 0 if d == 1 else 2)
 
         step = 0 if d == 1 else 2
         put(step * 3 + 1, chunk_product(1, 0 if d == 1 else HALO + FINE, d))
@@ -323,6 +327,7 @@
             def _():
                 to_rows(d, side).wait_recv()
                 to_rows_id(d, side).wait_recv()
+                spread_ids(side, 0 if d == 1 else 2)
 
             step = 0 if d == 1 else 2
             put(step * 3 + side, chunk_product(side, 0 if d == 1 else HALO + FINE, side // 2))
@@ -382,6 +387,7 @@
             pltpu.VMEM((LIVE, TILE, TILE), bf16),
             pltpu.VMEM((3, SPAN, P_TILES, TILE, TILE), bf16),
             pltpu.VMEM((3, SPAN * P_TILES, TILE), f32),
+            pltpu.VMEM((3, 3, 8, TILE), f32),
             pltpu.VMEM((FINE, WIDE_M, TILE), bf16),
             pltpu.VMEM((LIVE + 1, WIDE_M, TILE), bf16),
             pltpu.VMEM((2, HALO * TILE, WIDE_M), bf16),

time: 33.1 us -> 32.6 us (0.985)
  Pallas kernels: 30.8 us -> 30.3 us
    pallas_call x1, Pallas kernels: 30.8 us -> 30.3 us  [body(): pl.pallas_call(functools.partial(kernel, n_rows, n_wide), out_shape=pltpu...]
where the time goes in v4:
time: 32.6 us; the launch traced here: 32.5 us
  Pallas kernels  30.3 us (93%)
  local copies, waits for them, and re-layouts  2.19 us (7%)
    pallas_call x1, Pallas kernels, body(): pl.pallas_call(functools.partial(kernel, n_rows, n_wide), out_shape=pltpu...  30.3 us
    unnamed x1, local copies, waits for them, and re-layouts  2.19 us

profile of v4, /device:TPU:111, one launch (start us, length us, event | category | flops | bytes accessed | tf_op | source)
XLA Modules:
  0.0 32.5 jit_solution(17654517759736015283)
XLA Ops:
  0.0 30.3 %galerkin.1 = bf16[4,1,36,128,128]{4,3,2,1,0:T(8,128)(2,1)S(1)} custom-call(s32[17]{0:T(128)} %bitcast.6, s32[2,16]{1,0:T(2,128)} %bitcast.5, s32[1,128]{1,0:T(1,128)} %bitcast.7, bf16[128,1,128,128]{3,2,1,0:T(8,128)(2,1)} %a_hbm.1, bf16[16,1,2,128,128]{4,3,2,1,0:T(8,128)(2,1)} %p_hbm.1), custom_call_target="tpu_custom_call" | custom-call | tf_op jit(solution)/shard_map/galerkin/pallas_call | solution.py:381
  30.3 2.2 %copy.7 = bf16[4,1,36,128,128]{4,3,2,1,0:T(8,128)(2,1)} copy(bf16[4,1,36,128,128]{4,3,2,1,0:T(8,128)(2,1)S(1)} %galerkin.1) | data formatting | bytes 9437184

commit v5 on v4

--- a/solution.py
+++ b/solution.py
@@ -16,7 +16,7 @@
 LIVE = 112
 SPAN = FINE + 2 * HALO
 WIDE_M = COARSE * TILE
-PIECES = ((0, 4), (12, 4), (4, 4), (8, 2), (10, 2))
+PIECES = ((0, 4), (12, 4), (4, 4), (8, 3), (11, 1))
 MESH = pl.DeviceIdType.MESH
 
 
@@ -284,13 +284,15 @@
             def _():
                 if step == 0:
                     to_wide_id(d).wait_recv()
-                    spread_ids(side, 1)
                 to_wide(d, step).wait_recv()
 
                 @pl.when(has_row[step])
                 def _():
                     to_rows_id(step, side).start()
                     to_rows(step, side).start()
+
+                if step == 0:
+                    spread_ids(side, 1)
 
         for d in (0, 1):
             side = 0 if d == 1 else 2

time: 32.6 us -> 32.5 us (level)
  no operation moved by 1% of the time
where the time goes in v5:
time: 32.5 us; the launch traced here: 32.4 us
  Pallas kernels  30.2 us (93%)
  local copies, waits for them, and re-layouts  2.19 us (7%)
    pallas_call x1, Pallas kernels, body(): pl.pallas_call(functools.partial(kernel, n_rows, n_wide), out_shape=pltpu...  30.2 us
    unnamed x1, local copies, waits for them, and re-layouts  2.19 us

profile of v5, /device:TPU:111, one launch (start us, length us, event | category | flops | bytes accessed | tf_op | source)
XLA Modules:
  0.0 32.4 jit_solution(9973674893858234141)
XLA Ops:
  0.0 30.2 %galerkin.1 = bf16[4,1,36,128,128]{4,3,2,1,0:T(8,128)(2,1)S(1)} custom-call(s32[17]{0:T(128)} %bitcast.6, s32[2,16]{1,0:T(2,128)} %bitcast.5, s32[1,128]{1,0:T(1,128)} %bitcast.7, bf16[128,1,128,128]{3,2,1,0:T(8,128)(2,1)} %a_hbm.1, bf16[16,1,2,128,128]{4,3,2,1,0:T(8,128)(2,1)} %p_hbm.1), custom_call_target="tpu_custom_call" | custom-call | tf_op jit(solution)/shard_map/galerkin/pallas_call | solution.py:383
  30.2 2.2 %copy.7 = bf16[4,1,36,128,128]{4,3,2,1,0:T(8,128)(2,1)} copy(bf16[4,1,36,128,128]{4,3,2,1,0:T(8,128)(2,1)S(1)} %galerkin.1) | data formatting | bytes 9437184
